TPU v7x, 8 devices: a whole 2x2x1 slice. The times are simulated.
8 devices in a mesh: tp: 2 (over z, y), dp: 4 (over x, core).
Axes of the slice: x: 2, y: 2, z: 1, core: 2. Of those that a mesh axis runs over, the one named last changes fastest.
Arguments:
- x: bfloat16 [8192, 5120], P(('dp', 'tp'))
- w_gate: bfloat16 [5120, 14336], P('dp', 'tp')
- w_up: bfloat16 [5120, 14336], P('dp', 'tp')
- w_down: bfloat16 [14336, 5120], P('tp', 'dp')
Outputs:
- output: bfloat16 [8192, 5120], P(('dp', 'tp'))
All inputs are finite; a program needn't handle non-finite values.
Results may differ from a plain program's by a relative error of at most 0.0130042.
Values are sent between devices in bfloat16 or wider.
A program may use at most 1 GiB of HBM per device.

v0:
```python
import jax
import jax.numpy as jnp
from jax import lax
from jax.experimental import pallas as pl
from jax.experimental.pallas import tpu as pltpu
from jax.sharding import PartitionSpec as P

CW = 256


def late_chunks(nch):
    return min(4, nch // 3)


def kernel(x, wg, wu, wd, wv, w1, w2, w3, db, hb, po, rdi, r1i, yxi, hy, hx, wx,
           xb, hst, s_loc, s_xs, s_ws, s_xx, s_xy, s_xd, s_w1, s_w2, s_w3, s_d1, s_d2, s_d3, s_wx, s_hx,
           s_wv, s_h, s_po, s_rs, s_rd, s_r1, s_yx, s_ys, s_ld):
    rows, dim = x.shape
    dk = dim // 4
    fq = wg.shape[1] // 2
    nch = fq // CW
    first = nch // 2
    nl = late_chunks(nch)
    ne = nch - nl
    last = nch - 1
    ns = dk // CW
    f32, bf16 = jnp.float32, jnp.bfloat16

    t = lax.axis_index("tp")
    d = lax.axis_index("dp")
    side = d // 2
    core = d % 2
    mate = d + 1 - 2 * core
    quarter = [d, mate, (d + 2) % 4, (mate + 2) % 4]
    to_mate = {"dp": mate}
    to_x = {"dp": (d + 2) % 4}
    to_y = {"tp": 1 - t}

    def col(v, size=128):
        return v if isinstance(v, int) else pl.multiple_of(v, size)

    def send(src, dst, send_sem, recv_sem, where):
        pltpu.make_async_remote_copy(
            src_ref=src, dst_ref=dst, send_sem=send_sem, recv_sem=recv_sem,
            device_id=where, device_id_type=pl.DeviceIdType.MESH).start()

    def load(src, dst, sem):
        pltpu.make_async_copy(src, dst, sem).start()

    def wait(ref, sem):
        pltpu.make_async_copy(ref, ref, sem).wait()

    def block(b):
        return pl.ds(col(b * rows, rows), rows)

    def slot(s):
        return pl.ds(s * dk, dk)

    def piece(k):
        return pl.ds(col(k * CW), CW)

    barrier = pltpu.get_barrier_semaphore()
    for where in (to_mate, to_x, to_y):
        pl.semaphore_signal(barrier, inc=1, device_id=where, device_id_type=pl.DeviceIdType.MESH)
    pl.semaphore_wait(barrier, 3)

    own_cols = [pl.ds(col(quarter[s] * dk), dk) for s in range(4)]
    for s in range(4):
        src = x.at[:, own_cols[s]]
        send(src, xb.at[block(2), slot(s ^ 2)], s_xs.at[0], s_xx.at[s ^ 2], to_x)
        send(src, xb.at[block(1), slot(s)], s_xs.at[1], s_xy, to_y)
    for s in range(4):
        load(x.at[:, own_cols[s]], xb.at[block(0), slot(s)], s_loc)

    def send_chunk(j, _):
        for m, w in enumerate((wg, wu)):
            away = w.at[:, pl.ds(col((1 - side) * fq + j * CW), CW)]
            here = w.at[:, pl.ds(col(side * fq + j * CW), CW)]
            send(away, w2.at[j, :, pl.ds(m * CW, CW)], s_ws.at[1], s_w2.at[j], to_x)
            send(here, w1.at[j, :, pl.ds(m * CW, CW)], s_ws.at[0], s_w1, to_mate)
        return 0

    lax.fori_loop(0, nch, send_chunk, 0)

    def send_strip(k, _):
        send(wd.at[pl.ds(col((1 - side) * fq), fq), piece(k)], db.at[1, k], s_ws.at[3], s_d2.at[k], to_x)
        send(wd.at[pl.ds(col(side * fq), fq), piece(k)], db.at[0, k], s_ws.at[2], s_d1, to_mate)
        return 0

    lax.fori_loop(0, ns, send_strip, 0)

    for s in (2, 3, 0, 1):
        part = xb.at[block(2), slot(s)]
        wait(part, s_xx.at[s])
        send(part, xb.at[block(3), slot(s)], s_xs.at[2], s_xd, to_y)

    def send_rest(k, _):
        send(wd.at[pl.ds(col(side * fq + ne * CW), nl * CW), piece(k)], wx.at[0, k], s_ws.at[6], s_wx.at[0], to_y)
        return 0

    lax.fori_loop(0, ns, send_rest, 0)

    at_hand, to_come = pl.ds(0, 2 * dk), pl.ds(2 * dk, 2 * dk)

    def load_here(j, p, sem):
        for m, w in enumerate((wg, wu)):
            here = w.at[:, pl.ds(col(side * fq + j * CW), CW)]
            load(here, wv.at[p, slot(0), pl.ds(m * CW, CW)], s_wv.at[sem])

    def load_slot(w, j, n, p, sem):
        load(w.at[j], wv.at[p, slot(n)], s_wv.at[sem])

    def load_chunk(j, p):
        load_here(j, p, p)
        for n, w in ((1, w1), (2, w2), (3, w3)):
            load_slot(w, j, n, p, p)

    def load_local(j):
        load_here(j, 0, 3)
        load_slot(w1, j, 1, 0, 3)

    def fetch_chunk(j):
        wait(w2.at[j], s_w2.at[j])
        send(w2.at[j], w3.at[j], s_ws.at[4], s_w3.at[j], to_mate)
        load_slot(w2, j, 2, 0, 0)
        wait(w3.at[j], s_w3.at[j])
        load_slot(w3, j, 3, 0, 0)

    def wait_chunk():
        wait(wv.at[0, at_hand, :], s_wv.at[3])
        wait(wv.at[0, to_come, :], s_wv.at[0])

    def hcopy(b, j, q):
        return pltpu.make_async_copy(hst.at[q], hb.at[block(b), piece(j)], s_h.at[q])

    def gated(b, p):
        ab = jnp.dot(xb[block(b), :], wv[p], preferred_element_type=f32)
        a = ab[:, :CW]
        return (a * jax.nn.sigmoid(a) * ab[:, CW:]).astype(bf16)

    def gate(b, j, p, q, used=True, to=None):
        to = b if to is None else to

        @pl.when(used)
        def _():
            hcopy(to, j, q).wait()

        hst[q] = gated(b, p)
        hcopy(to, j, q).start()

    wait(xb.at[block(0), :], s_loc)
    wait(xb.at[block(1), :], s_xy)
    wait(w1, s_w1)
    load_local(0)

    hcols = pl.ds(0, fq)
    ecols = pl.ds(0, ne * CW)
    both = pl.ds(fq, 2 * CW)

    def load_h(b, to):
        load(hb.at[block(b), :], xb.at[block(to), hcols], s_ld.at[to])

    def wait_h(to):
        wait(xb.at[block(to), hcols], s_ld.at[to])

    def tile(b, c, n=1):
        return xb.at[block(b), pl.ds(fq + c * CW, n * CW)]

    halves = (pl.ds(0, CW), pl.ds(CW, CW))

    def load_early(k, p):
        load(wd.at[pl.ds(col(side * fq), ne * CW), piece(k)], wv.at[p, ecols, halves[0]], s_wv.at[p])
        load(db.at[0, k, ecols, :], wv.at[p, ecols, halves[1]], s_wv.at[p])

    def load_pair(half, k, p):
        if half == 0:
            src = (wd.at[pl.ds(col(side * fq), fq), piece(k)], db.at[0, k])
        else:
            src = (db.at[1, k], db.at[2, k])
        for m in range(2):
            load(src[m], wv.at[p, hcols, halves[m]], s_wv.at[p])

    def wait_pair(p):
        wait(wv.at[p, hcols, :], s_wv.at[p])

    def put(b, out, u):
        for m in range(2):
            load(tile(b, m), po.at[out, u, m], s_po)
        wait(tile(b, 0, 2), s_po)

    def down(b, out, u, p):
        o = jnp.dot(xb[block(b), hcols], wv[p, hcols, :], preferred_element_type=f32)
        xb[block(b), both] = o.astype(bf16)
        put(b, out, u)

    def ship_d(u):
        for m in range(2):
            send(po.at[3, u, m], rdi.at[u, m], s_rs.at[0], s_rd.at[u], to_y)

    def ship_1(u):
        for m in range(2):
            send(po.at[1, u, m], r1i.at[u, m], s_rs.at[1], s_r1.at[u], to_y)

    def chunk(j, _):
        fetch_chunk(j)

        @pl.when(j == first)
        def _():
            wait(xb.at[block(3), :], s_xd)

        @pl.when(j >= first)
        def _():
            load_chunk(j - first, 1)

        wait_chunk()

        def rows_of(n, _):
            g = 3 * j + n
            gate((n + 1) % 3, j, 0, g % 2, g >= 2)
            return 0

        lax.fori_loop(0, 3, rows_of, 0)
        load_local(j + 1)

        @pl.when(j + 1 == ne)
        def _():
            for n in range(2):
                hcopy(0, 0, n).wait()
            load(hb.at[block(1), ecols], xb.at[block(0), ecols], s_ld.at[0])
            wait(db.at[0], s_d1)
            load_early(0, 2)

        @pl.when(j >= first)
        def _():
            wait(wv.at[1], s_wv.at[1])
            gate(3, j - first, 1, 2, j > first)

        return 0

    lax.fori_loop(0, ne, chunk, 0)

    wait(xb.at[block(0), ecols], s_ld.at[0])

    def early(k, _):
        p = 2 - k % 2

        @pl.when(k + 1 < ns)
        def _():
            load_early(k + 1, 3 - p)

        wait(wv.at[p, ecols, :], s_wv.at[p])
        o = jnp.dot(xb[block(0), ecols], wv[p, ecols, :], preferred_element_type=f32)
        xb[block(0), both] = o.astype(bf16)
        put(0, 1, k)
        ship_1(k)
        return 0

    lax.fori_loop(0, ns, early, 0)

    done = ne - first + 2 * (nl - 2)

    def late(j, _):
        fetch_chunk(j)
        two = (j > ne) & (j < last)
        base = ne - first + 2 * (j - ne - 1)

        @pl.when(two)
        def _():
            for i in range(2):
                load_chunk(base + i, 1 + i)

        @pl.when(j == last)
        def _():
            load_chunk(done, 1)

        wait_chunk()
        hst[0] = gated(1, 0)
        load(hst.at[0], hy.at[j - ne], s_h.at[0])
        gate(2, j, 0, 1, j > ne)
        wait(hst.at[0], s_h.at[0])
        send(hy.at[j - ne], hx.at[j - ne], s_rs.at[2], s_hx, to_y)

        @pl.when(j < last)
        def _():
            load_local(j + 1)

        @pl.when(two)
        def _():
            def old(i, _):
                wait(wv.at[1 + i], s_wv.at[1 + i])
                gate(3, base + i, 1 + i, 2)
                return 0

            lax.fori_loop(0, 2, old, 0)

        return 0

    lax.fori_loop(ne, nch, late, 0)
    for j in range(nl):
        load(hy.at[j], xb.at[block(0), pl.ds((ne + j) * CW, CW)], s_ld.at[0])
    hcopy(2, last, 1).wait()
    wait(xb.at[block(2), :], s_xs.at[2])
    load_h(2, 2)
    wait(wx.at[0], s_wx.at[0])
    send(wx.at[0], wx.at[1], s_ws.at[7], s_wx.at[1], to_mate)

    def diagonal(j, _):
        i = j - done
        p = jnp.where(j == last, 0, 1 + i % 2)

        @pl.when(j + 1 < last)
        def _():
            load_chunk(j + 1, 2 - i % 2)

        @pl.when(j < last)
        def _():
            wait(wv.at[p], s_wv.at[p])

        gate(3, j, p, 2 - i % 2, i != 1)
        return 0

    lax.fori_loop(done, nch, diagonal, 0)
    load_pair(0, 0, 1)
    for q in (1, 2):
        hcopy(3, last, q).wait()
    load_h(3, 3)
    wait(xb.at[block(0), pl.ds(ne * CW, nl * CW)], s_ld.at[0])
    wait_h(2)
    wait_h(3)
    for s in range(4):
        load(x.at[:, own_cols[s]], xb.at[block(1), slot(s)], s_loc)

    def forward_strip(k):
        wait(db.at[1, k], s_d2.at[k])
        send(db.at[1, k], db.at[2, k], s_ws.at[5], s_d3.at[k], to_mate)

    def own_half(k, _):
        p = 1 + k % 2

        @pl.when(k + 1 < ns)
        def _():
            load_pair(0, k + 1, 3 - p)

        wait_pair(p)

        def rows_of(n, _):
            down(3 - n, 3 - n, k, p)

            @pl.when(n == 0)
            def _():
                ship_d(k)

            return 0

        lax.fori_loop(0, 2, rows_of, 0)

        @pl.when(k == 1)
        def _():
            forward_strip(0)

        @pl.when(k + 1 == ns)
        def _():
            forward_strip(1)

        return 0

    lax.fori_loop(0, ns, own_half, 0)

    def total(tiles):
        o = xb[block(tiles[0][0]), pl.ds(fq + tiles[0][1] * CW, CW)].astype(f32)
        for b, c in tiles[1:]:
            o = o + xb[block(b), pl.ds(fq + c * CW, CW)].astype(f32)
        return o.astype(bf16)

    def ring_at(ring, m):
        b = jnp.where(ring == 0, 0, jnp.where(ring == 3, 3, 2))
        c = jnp.where(ring == 1, 2, 4)
        return block(b), pl.ds(col(fq + (c + m) * CW), CW)

    def ring_tile(ring, m):
        return xb.at[ring_at(ring, m)]

    def relay(half, k, m, turn):
        u = half * ns + k
        load(po.at[2, u, m], tile(0, 2), s_ld.at[0])
        if m == 0:
            wait(rdi.at[u], s_rd.at[u])
        load(rdi.at[u, m], tile(0, 3), s_ld.at[1])
        ring = turn % 4

        @pl.when(turn >= 4)
        def _():
            wait(ring_tile(ring, m), s_ys.at[2 * ring + m])

        wait(tile(0, 2), s_ld.at[0])
        wait(tile(0, 3), s_ld.at[1])
        xb[ring_at(ring, m)] = total(((0, 2), (0, 3)))
        v = (1 - half) * ns + k
        sem = v if m == 0 else jnp.where(v == ns - 1, 2 * ns, v)
        send(ring_tile(ring, m), yxi.at[v, m], s_ys.at[2 * ring + m], s_yx.at[sem], to_x)

    def fetch_pair(k):
        @pl.when(k >= 3)
        def _():
            forward_strip(k)

        wait(db.at[2, k], s_d3.at[k])
        load_pair(1, k, 1 + k % 2)

    def other_half(k, _):
        p = 1 + k % 2
        u = ns + k
        wait_pair(p)

        def rows_of(n, _):
            b = jnp.where(n == 0, 3, jnp.where(n == 1, 0, 2))
            down(b, jnp.where(n == 1, 1, b), u, p)

            @pl.when(n == 0)
            def _():
                ship_d(u)

            @pl.when((n == 1) & (k > 0))
            def _():
                ship_1(u - 1)

            return 0

        lax.fori_loop(0, 3, rows_of, 0)
        for m in range(2):
            relay(0, k, m, k)

        @pl.when(k == 0)
        def _():
            forward_strip(2)

        @pl.when(k + 1 < ns)
        def _():
            fetch_pair(k + 1)

        return 0

    fetch_pair(0)
    lax.fori_loop(0, ns, other_half, 0)
    ship_1(2 * ns - 1)

    load_chunk(ne, 1)
    wait(xb.at[block(1), :], s_loc)

    def own_late(j, _):
        i = j - ne
        p = jnp.where(j == last, 0, 1 + i % 2)

        @pl.when(j + 1 < last)
        def _():
            load_chunk(j + 1, 2 - i % 2)

        @pl.when(j < last)
        def _():
            wait(wv.at[p], s_wv.at[p])

        gate(1, j, p, i % 2, i > 1, 0)
        return 0

    lax.fori_loop(ne, nch, own_late, 0)

    long = pl.ds(0, fq + nl * CW)
    rest = pl.ds(fq, nl * CW)

    def load_long(k, p):
        load_pair(0, k, p)
        for m in range(2):
            load(wx.at[m, k], wv.at[p, rest, halves[m]], s_wv.at[p])

    for q in range(2):
        hcopy(0, last, q).wait()
    load_h(0, 1)
    wait(hx, s_hx)
    for j in range(nl):
        load(hx.at[j], xb.at[block(1), pl.ds(fq + j * CW, CW)], s_ld.at[3])
    wait(wx.at[1], s_wx.at[1])
    load_long(0, 1)
    wait_h(1)
    wait(xb.at[block(1), rest], s_ld.at[3])

    for m in range(2):
        relay(1, 0, m, ns)

    def own_rows(k, _):
        p = 1 + k % 2

        @pl.when(k + 1 < ns)
        def _():
            load_long(k + 1, 3 - p)

        wait(wv.at[p, long, :], s_wv.at[p])
        o = jnp.dot(xb[block(1), long], wv[p, long, :], preferred_element_type=f32)
        xb[block(0), both] = o.astype(bf16)
        put(0, 0, k)
        return 0

    lax.fori_loop(0, ns, own_rows, 0)
    load_pair(1, 0, 1)
    for m in range(2):
        relay(1, 1, m, ns + 1)

    def own_rows_too(k, _):
        p = 1 + k % 2

        @pl.when(k + 1 < ns)
        def _():
            load_pair(1, k + 1, 3 - p)

        wait_pair(p)
        down(1, 0, ns + k, p)
        return 0

    lax.fori_loop(0, ns, own_rows_too, 0)
    for m in range(2):
        relay(1, 2, m, ns + 2)

    parts = ((1, 2), (1, 3), (1, 4), (1, 5))

    def keep(half, k, m, o):
        wv[half, pl.ds(col(k * rows, rows), rows), halves[m]] = o

    def finish(half, k, m):
        u = half * ns + k
        n = 2 * half + m
        cols = pl.ds(col(quarter[n] * dk + k * CW), CW)
        load(po.at[0, u, m], tile(*parts[0]), s_ld.at[0])
        load(x.at[:, cols], tile(*parts[1]), s_ld.at[1])
        if m == 0:
            wait(r1i.at[u], s_r1.at[u])
        load(r1i.at[u, m], tile(*parts[2]), s_ld.at[2])
        if m == 0 and half == 1:
            wait(yxi.at[u], s_yx.at[u])
        if m == 0 and half == 0:
            @pl.when(k + 1 < ns)
            def _():
                wait(yxi.at[u], s_yx.at[u])

            @pl.when(k + 1 == ns)
            def _():
                wait(yxi.at[u, 0], s_yx.at[u])
        load(yxi.at[u, m], tile(*parts[3]), s_ld.at[3])
        for c in range(4):
            wait(tile(*parts[c]), s_ld.at[c])
        keep(half, k, m, total(parts))

    def begin():
        load(po.at[0, ns - 1, 1], tile(*parts[0]), s_ld.at[0])
        load(r1i.at[ns - 1, 1], tile(*parts[1]), s_ld.at[1])
        wait(tile(*parts[0]), s_ld.at[0])
        wait(tile(*parts[1]), s_ld.at[1])
        keep(0, ns - 1, 1, total(parts[:2]))

    def tail(k, _):
        @pl.when((k > 2) & (k < ns))
        def _():
            for m in range(2):
                relay(1, k, m, ns + k)

        @pl.when(k > 0)
        def _():
            finish(0, k - 1, 0)

            @pl.when(k < ns)
            def _():
                finish(0, k - 1, 1)

            @pl.when(k == ns)
            def _():
                begin()

            for m in range(2):
                finish(1, k - 1, m)

        return 0

    lax.fori_loop(0, ns + 1, tail, 0)

    for m in range(2):
        for ring in range(4):
            wait(ring_tile(ring, m), s_ys.at[2 * ring + m])
    wait(x, s_xs.at[0])
    wait(x, s_xs.at[1])
    wait(w1, s_ws.at[0])
    wait(w2, s_ws.at[1])
    wait(db.at[0], s_ws.at[2])
    wait(db.at[1], s_ws.at[3])
    wait(w3, s_ws.at[4])
    wait(db.at[2], s_ws.at[5])
    wait(wx.at[0], s_ws.at[6])
    wait(wx.at[1], s_ws.at[7])
    wait(rdi, s_rs.at[0])
    wait(r1i, s_rs.at[1])
    wait(hx, s_rs.at[2])
    wait(yxi.at[ns - 1, 1], s_yx.at[2 * ns])


def write(x, done, yxi, y, strip, s_in, s_out):
    rows, dim = x.shape
    dk = dim // 4
    ns = dk // CW
    d = lax.axis_index("dp")
    mate = d + 1 - 2 * (d % 2)
    quarter = [d, mate, (d + 2) % 4, (mate + 2) % 4]

    def cols(half, k, m):
        return pl.ds(pl.multiple_of(quarter[2 * half + m] * dk + k * CW, 128), CW)

    def kept(half, k, m):
        return done.at[half, pl.ds(k * rows, rows), pl.ds(m * CW, CW)]

    end = (0, ns - 1, 1)
    loads = [pltpu.make_async_copy(src, strip.at[i], s_in.at[i])
             for i, src in enumerate((x.at[:, cols(*end)], yxi.at[ns - 1, 1]))]
    for copy in loads:
        copy.start()
    strips = [(half, k, m) for k in range(ns) for half in range(2) for m in range(2)]
    strips.remove(end)
    outs = [pltpu.make_async_copy(kept(*i), y.at[:, cols(*i)], s_out.at[n]) for n, i in enumerate(strips)]
    for copy in outs:
        copy.start()
    for copy in loads:
        copy.wait()
    o = kept(*end)[...].astype(jnp.float32) + strip[1].astype(jnp.float32) + strip[0].astype(jnp.float32)
    strip[2] = o.astype(strip.dtype)
    outs.append(pltpu.make_async_copy(strip.at[2], y.at[:, cols(*end)], s_out.at[len(strips)]))
    outs[-1].start()
    for copy in outs:
        copy.wait()


def solution(mesh):
    def body(x, wg, wu, wd):
        rows, dim = x.shape
        dk = dim // 4
        fq = wg.shape[1] // 2
        nch = fq // CW
        nl = late_chunks(nch)
        ns = dk // CW
        bf16 = jnp.bfloat16
        dma = pltpu.SemaphoreType.DMA
        pairs = (2 * ns, 2, rows, CW)
        shapes = [
            (nch, dk, 2 * CW), (nch, dk, 2 * CW), (nch, dk, 2 * CW),
            (3, ns, fq, CW),
            (4 * rows, fq),
            (4,) + pairs, pairs, pairs, pairs,
            (nl, rows, CW), (nl, rows, CW),
            (2, ns, nl * CW, CW),
        ]
        any_space = pl.BlockSpec(memory_space=pl.ANY)
        in_vmem = pl.BlockSpec(memory_space=pltpu.VMEM)
        outs = pl.pallas_call(
            kernel,
            out_shape=[pltpu.VMEM((3, dim, 2 * CW), bf16)] + [jax.ShapeDtypeStruct(s, bf16) for s in shapes],
            in_specs=[any_space] * 4,
            out_specs=[in_vmem] + [any_space] * len(shapes),
            scratch_shapes=[
                pltpu.VMEM((4 * rows, dim), bf16),
                pltpu.VMEM((3, rows, CW), bf16),
                dma, dma((3,)), dma((8,)), dma((4,)), dma, dma,
                dma, dma((nch,)), dma((nch,)), dma, dma((ns,)), dma((ns,)), dma((2,)), dma,
                dma((4,)), dma((3,)), dma, dma((3,)),
                dma((2 * ns,)), dma((2 * ns,)), dma((2 * ns + 1,)), dma((8,)), dma((4,)),
            ],
            compiler_params=pltpu.CompilerParams(
                collective_id=0, has_side_effects=True, vmem_limit_bytes=48 * 2**20),
            cost_estimate=pl.CostEstimate(
                flops=6 * rows * 4 * dim * fq, bytes_accessed=4 * rows * dim * 2, transcendentals=0),
        )(x, wg, wu, wd)
        return pl.pallas_call(
            write,
            out_shape=jax.ShapeDtypeStruct((rows, dim), bf16),
            in_specs=[any_space, in_vmem, any_space],
            out_specs=any_space,
            scratch_shapes=[pltpu.VMEM((3, rows, CW), bf16), dma((2,)), dma((4 * ns,))],
            compiler_params=pltpu.CompilerParams(vmem_limit_bytes=48 * 2**20),
        )(x, pltpu.with_memory_space_constraint(outs[0], pltpu.VMEM), outs[9])

    return jax.shard_map(body, mesh=mesh, in_specs=(P(("dp", "tp"), None), P("dp", "tp"), P("dp", "tp"), P("tp", "dp")), out_specs=P(("dp", "tp"), None), check_vma=False)
```

profile of v0, /device:TPU:0, one launch (start us, length us, event | category | flops | bytes accessed | tf_op | source)
XLA Modules:
  0.0 1049.9 jit_solution(11729932316495925294)
XLA Ops:
  0.0 1045.6 %shard_map.46 = (bf16[3,5120,512]{2,1,0:T(8,128)(2,1)S(1)}, bf16[14,1280,512]{2,1,0:T(8,128)(2,1)}, bf16[14,1280,512]{2,1,0:T(8,128)(2,1)}, bf16[14,1280,512]{2,...) custom-call(bf16[1024,5120]{1,0:T(8,128)(2,1)} %x.3, ...), custom_call_target="tpu_custom_call" | custom-call | flops 450971566080 | bytes 41943040 | tf_op jit(solution)/shard_map/pallas_call | solution.py:657
  1045.6 4.1 shard_map.47
where the time goes:
time: 1050 us
  Pallas kernels  1050 us (100%)
    pallas_call x1, Pallas kernels, body(): pl.pallas_call(kernel, out_shape=[pltpu.VMEM((3, dim, 2 * CW), bf16)] + [...  1050 us

commit v1 on v0

--- a/solution.py
+++ b/solution.py
@@ -197,9 +197,9 @@
         for m in range(2):
             send(po.at[3, u, m], rdi.at[u, m], s_rs.at[0], s_rd.at[u], to_y)
 
-    def ship_1(u):
+    def ship_1(u, n):
         for m in range(2):
-            send(po.at[1, u, m], r1i.at[u, m], s_rs.at[1], s_r1.at[u], to_y)
+            send(po.at[1, u, m], r1i.at[u, m], s_rs.at[1], s_r1.at[n], to_y)
 
     def chunk(j, _):
         fetch_chunk(j)
@@ -252,7 +252,7 @@
         o = jnp.dot(xb[block(0), ecols], wv[p, ecols, :], preferred_element_type=f32)
         xb[block(0), both] = o.astype(bf16)
         put(0, 1, k)
-        ship_1(k)
+        ship_1(k, 0)
         return 0
 
     lax.fori_loop(0, ns, early, 0)
@@ -372,13 +372,13 @@
             o = o + xb[block(b), pl.ds(fq + c * CW, CW)].astype(f32)
         return o.astype(bf16)
 
-    def ring_at(ring, m):
+    def ring_at(ring, m, n=1):
         b = jnp.where(ring == 0, 0, jnp.where(ring == 3, 3, 2))
         c = jnp.where(ring == 1, 2, 4)
-        return block(b), pl.ds(col(fq + (c + m) * CW), CW)
-
-    def ring_tile(ring, m):
-        return xb.at[ring_at(ring, m)]
+        return block(b), pl.ds(col(fq + (c + m) * CW), n * CW)
+
+    def ring_tile(ring, m, n=1):
+        return xb.at[ring_at(ring, m, n)]
 
     def relay(half, k, m, turn):
         u = half * ns + k
@@ -388,16 +388,16 @@
         load(rdi.at[u, m], tile(0, 3), s_ld.at[1])
         ring = turn % 4
 
-        @pl.when(turn >= 4)
-        def _():
-            wait(ring_tile(ring, m), s_ys.at[2 * ring + m])
+        @pl.when((turn >= 4) & (m == 0))
+        def _():
+            wait(ring_tile(ring, 0, 2), s_ys.at[ring])
 
         wait(tile(0, 2), s_ld.at[0])
         wait(tile(0, 3), s_ld.at[1])
         xb[ring_at(ring, m)] = total(((0, 2), (0, 3)))
         v = (1 - half) * ns + k
-        sem = v if m == 0 else jnp.where(v == ns - 1, 2 * ns, v)
-        send(ring_tile(ring, m), yxi.at[v, m], s_ys.at[2 * ring + m], s_yx.at[sem], to_x)
+        sem = 0 if half == 0 else k + 1 if m == 0 else jnp.where(k + 1 == ns, ns + 1, k + 1)
+        send(ring_tile(ring, m), yxi.at[v, m], s_ys.at[ring], s_yx.at[sem], to_x)
 
     def fetch_pair(k):
         @pl.when(k >= 3)
@@ -422,7 +422,7 @@
 
             @pl.when((n == 1) & (k > 0))
             def _():
-                ship_1(u - 1)
+                ship_1(u - 1, k)
 
             return 0
 
@@ -442,7 +442,7 @@
 
     fetch_pair(0)
     lax.fori_loop(0, ns, other_half, 0)
-    ship_1(2 * ns - 1)
+    ship_1(2 * ns - 1, ns)
 
     load_chunk(ne, 1)
     wait(xb.at[block(1), :], s_loc)
@@ -530,19 +530,17 @@
         cols = pl.ds(col(quarter[n] * dk + k * CW), CW)
         load(po.at[0, u, m], tile(*parts[0]), s_ld.at[0])
         load(x.at[:, cols], tile(*parts[1]), s_ld.at[1])
-        if m == 0:
-            wait(r1i.at[u], s_r1.at[u])
+        if m == 0 and half == 1:
+            wait(r1i.at[u], s_r1.at[k + 1])
         load(r1i.at[u, m], tile(*parts[2]), s_ld.at[2])
-        if m == 0 and half == 1:
-            wait(yxi.at[u], s_yx.at[u])
         if m == 0 and half == 0:
             @pl.when(k + 1 < ns)
             def _():
-                wait(yxi.at[u], s_yx.at[u])
+                wait(yxi.at[u], s_yx.at[k + 1])
 
             @pl.when(k + 1 == ns)
             def _():
-                wait(yxi.at[u, 0], s_yx.at[u])
+                wait(yxi.at[u, 0], s_yx.at[k + 1])
         load(yxi.at[u, m], tile(*parts[3]), s_ld.at[3])
         for c in range(4):
             wait(tile(*parts[c]), s_ld.at[c])
@@ -555,6 +553,9 @@
         wait(tile(*parts[1]), s_ld.at[1])
         keep(0, ns - 1, 1, total(parts[:2]))
 
+    wait(r1i.at[pl.ds(0, ns)], s_r1.at[0])
+    wait(yxi.at[pl.ds(ns, ns)], s_yx.at[0])
+
     def tail(k, _):
         @pl.when((k > 2) & (k < ns))
         def _():
@@ -580,9 +581,8 @@
 
     lax.fori_loop(0, ns + 1, tail, 0)
 
-    for m in range(2):
-        for ring in range(4):
-            wait(ring_tile(ring, m), s_ys.at[2 * ring + m])
+    for ring in range(4):
+        wait(ring_tile(ring, 0, 2), s_ys.at[ring])
     wait(x, s_xs.at[0])
     wait(x, s_xs.at[1])
     wait(w1, s_ws.at[0])
@@ -596,7 +596,7 @@
     wait(rdi, s_rs.at[0])
     wait(r1i, s_rs.at[1])
     wait(hx, s_rs.at[2])
-    wait(yxi.at[ns - 1, 1], s_yx.at[2 * ns])
+    wait(yxi.at[ns - 1, 1], s_yx.at[ns + 1])
 
 
 def write(x, done, yxi, y, strip, s_in, s_out):
@@ -620,17 +620,15 @@
         copy.start()
     strips = [(half, k, m) for k in range(ns) for half in range(2) for m in range(2)]
     strips.remove(end)
-    outs = [pltpu.make_async_copy(kept(*i), y.at[:, cols(*i)], s_out.at[n]) for n, i in enumerate(strips)]
+    outs = [pltpu.make_async_copy(kept(*i), y.at[:, cols(*i)], s_out) for i in strips]
     for copy in outs:
         copy.start()
     for copy in loads:
         copy.wait()
     o = kept(*end)[...].astype(jnp.float32) + strip[1].astype(jnp.float32) + strip[0].astype(jnp.float32)
     strip[2] = o.astype(strip.dtype)
-    outs.append(pltpu.make_async_copy(strip.at[2], y.at[:, cols(*end)], s_out.at[len(strips)]))
-    outs[-1].start()
-    for copy in outs:
-        copy.wait()
+    pltpu.make_async_copy(strip.at[2], y.at[:, cols(*end)], s_out).start()
+    pltpu.make_async_copy(y, y, s_out).wait()
 
 
 def solution(mesh):
@@ -665,7 +663,7 @@
                 dma, dma((3,)), dma((8,)), dma((4,)), dma, dma,
                 dma, dma((nch,)), dma((nch,)), dma, dma((ns,)), dma((ns,)), dma((2,)), dma,
                 dma((4,)), dma((3,)), dma, dma((3,)),
-                dma((2 * ns,)), dma((2 * ns,)), dma((2 * ns + 1,)), dma((8,)), dma((4,)),
+                dma((2 * ns,)), dma((ns + 1,)), dma((ns + 2,)), dma((4,)), dma((4,)),
             ],
             compiler_params=pltpu.CompilerParams(
                 collective_id=0, has_side_effects=True, vmem_limit_bytes=48 * 2**20),
@@ -677,7 +675,7 @@
             out_shape=jax.ShapeDtypeStruct((rows, dim), bf16),
             in_specs=[any_space, in_vmem, any_space],
             out_specs=any_space,
-            scratch_shapes=[pltpu.VMEM((3, rows, CW), bf16), dma((2,)), dma((4 * ns,))],
+            scratch_shapes=[pltpu.VMEM((3, rows, CW), bf16), dma((2,)), dma],
             compiler_params=pltpu.CompilerParams(vmem_limit_bytes=48 * 2**20),
         )(x, pltpu.with_memory_space_constraint(outs[0], pltpu.VMEM), outs[9])
 

time: 1050 us -> 1050 us (level)
  no operation moved by 1% of the time
where the time goes in v1:
time: 1050 us
  Pallas kernels  1050 us (100%)
    pallas_call x1, Pallas kernels, body(): pl.pallas_call(kernel, out_shape=[pltpu.VMEM((3, dim, 2 * CW), bf16)] + [...  1050 us

profile of v1, /device:TPU:0, one launch (start us, length us, event | category | flops | bytes accessed | tf_op | source)
XLA Modules:
  0.0 1049.6 jit_solution(9581915637744342472)
XLA Ops:
  0.0 1045.5 %shard_map.46 = (bf16[3,5120,512]{2,1,0:T(8,128)(2,1)S(1)}, bf16[14,1280,512]{2,1,0:T(8,128)(2,1)}, bf16[14,1280,512]{2,1,0:T(8,128)(2,1)}, bf16[14,1280,512]{2,...) custom-call(bf16[1024,5120]{1,0:T(8,128)(2,1)} %x.3, ...), custom_call_target="tpu_custom_call" | custom-call | flops 450971566080 | bytes 41943040 | tf_op jit(solution)/shard_map/pallas_call | solution.py:655
  1045.5 3.9 shard_map.47

commit v2 on v1

--- a/solution.py
+++ b/solution.py
@@ -121,9 +121,9 @@
 
     def fetch_chunk(j):
         wait(w2.at[j], s_w2.at[j])
-        send(w2.at[j], w3.at[j], s_ws.at[4], s_w3.at[j], to_mate)
+        send(w2.at[j], w3.at[j], s_ws.at[4], s_w3.at[j % 2], to_mate)
         load_slot(w2, j, 2, 0, 0)
-        wait(w3.at[j], s_w3.at[j])
+        wait(w3.at[j], s_w3.at[j % 2])
         load_slot(w3, j, 3, 0, 0)
 
     def wait_chunk():
@@ -332,7 +332,7 @@
 
     def forward_strip(k):
         wait(db.at[1, k], s_d2.at[k])
-        send(db.at[1, k], db.at[2, k], s_ws.at[5], s_d3.at[k], to_mate)
+        send(db.at[1, k], db.at[2, k], s_ws.at[5], s_d3.at[k % 3], to_mate)
 
     def own_half(k, _):
         p = 1 + k % 2
@@ -404,7 +404,7 @@
         def _():
             forward_strip(k)
 
-        wait(db.at[2, k], s_d3.at[k])
+        wait(db.at[2, k], s_d3.at[k % 3])
         load_pair(1, k, 1 + k % 2)
 
     def other_half(k, _):
@@ -547,11 +547,14 @@
         keep(half, k, m, total(parts))
 
     def begin():
+        spare_x = wv.at[2, pl.ds(0, rows), halves[0]]
+        load(x.at[:, pl.ds(col(quarter[1] * dk + (ns - 1) * CW), CW)], spare_x, s_ld.at[2])
         load(po.at[0, ns - 1, 1], tile(*parts[0]), s_ld.at[0])
         load(r1i.at[ns - 1, 1], tile(*parts[1]), s_ld.at[1])
         wait(tile(*parts[0]), s_ld.at[0])
         wait(tile(*parts[1]), s_ld.at[1])
         keep(0, ns - 1, 1, total(parts[:2]))
+        wait(spare_x, s_ld.at[2])
 
     wait(r1i.at[pl.ds(0, ns)], s_r1.at[0])
     wait(yxi.at[pl.ds(ns, ns)], s_yx.at[0])
@@ -599,8 +602,8 @@
     wait(yxi.at[ns - 1, 1], s_yx.at[ns + 1])
 
 
-def write(x, done, yxi, y, strip, s_in, s_out):
-    rows, dim = x.shape
+def write(done, yxi, y, strip, s_in, s_out):
+    rows, dim = y.shape
     dk = dim // 4
     ns = dk // CW
     d = lax.axis_index("dp")
@@ -614,20 +617,18 @@
         return done.at[half, pl.ds(k * rows, rows), pl.ds(m * CW, CW)]
 
     end = (0, ns - 1, 1)
-    loads = [pltpu.make_async_copy(src, strip.at[i], s_in.at[i])
-             for i, src in enumerate((x.at[:, cols(*end)], yxi.at[ns - 1, 1]))]
-    for copy in loads:
-        copy.start()
+    late = pltpu.make_async_copy(yxi.at[ns - 1, 1], strip.at[0], s_in)
+    late.start()
     strips = [(half, k, m) for k in range(ns) for half in range(2) for m in range(2)]
     strips.remove(end)
     outs = [pltpu.make_async_copy(kept(*i), y.at[:, cols(*i)], s_out) for i in strips]
     for copy in outs:
         copy.start()
-    for copy in loads:
-        copy.wait()
-    o = kept(*end)[...].astype(jnp.float32) + strip[1].astype(jnp.float32) + strip[0].astype(jnp.float32)
-    strip[2] = o.astype(strip.dtype)
-    pltpu.make_async_copy(strip.at[2], y.at[:, cols(*end)], s_out).start()
+    late.wait()
+    o = kept(*end)[...].astype(jnp.float32) + strip[0].astype(jnp.float32)
+    o = o + done[2, pl.ds(0, rows), pl.ds(0, CW)].astype(jnp.float32)
+    strip[1] = o.astype(strip.dtype)
+    pltpu.make_async_copy(strip.at[1], y.at[:, cols(*end)], s_out).start()
     pltpu.make_async_copy(y, y, s_out).wait()
 
 
@@ -661,7 +662,7 @@
                 pltpu.VMEM((4 * rows, dim), bf16),
                 pltpu.VMEM((3, rows, CW), bf16),
                 dma, dma((3,)), dma((8,)), dma((4,)), dma, dma,
-                dma, dma((nch,)), dma((nch,)), dma, dma((ns,)), dma((ns,)), dma((2,)), dma,
+                dma, dma((nch,)), dma((2,)), dma, dma((ns,)), dma((3,)), dma((2,)), dma,
                 dma((4,)), dma((3,)), dma, dma((3,)),
                 dma((2 * ns,)), dma((ns + 1,)), dma((ns + 2,)), dma((4,)), dma((4,)),
             ],
@@ -673,10 +674,10 @@
         return pl.pallas_call(
             write,
             out_shape=jax.ShapeDtypeStruct((rows, dim), bf16),
-            in_specs=[any_space, in_vmem, any_space],
+            in_specs=[in_vmem, any_space],
             out_specs=any_space,
-            scratch_shapes=[pltpu.VMEM((3, rows, CW), bf16), dma((2,)), dma],
+            scratch_shapes=[pltpu.VMEM((2, rows, CW), bf16), dma, dma],
             compiler_params=pltpu.CompilerParams(vmem_limit_bytes=48 * 2**20),
-        )(x, pltpu.with_memory_space_constraint(outs[0], pltpu.VMEM), outs[9])
+        )(pltpu.with_memory_space_constraint(outs[0], pltpu.VMEM), outs[9])
 
     return jax.shard_map(body, mesh=mesh, in_specs=(P(("dp", "tp"), None), P("dp", "tp"), P("dp", "tp"), P("tp", "dp")), out_specs=P(("dp", "tp"), None), check_vma=False)

time: 1050 us -> 1050 us (level)
  no operation moved by 1% of the time
where the time goes in v2:
time: 1050 us
  Pallas kernels  1050 us (100%)
    pallas_call x1, Pallas kernels, body(): pl.pallas_call(kernel, out_shape=[pltpu.VMEM((3, dim, 2 * CW), bf16)] + [...  1050 us

profile of v2, /device:TPU:0, one launch (start us, length us, event | category | flops | bytes accessed | tf_op | source)
XLA Modules:
  0.0 1049.5 jit_solution(13764436331724074047)
XLA Ops:
  0.0 1045.3 %shard_map.46 = (bf16[3,5120,512]{2,1,0:T(8,128)(2,1)S(1)}, bf16[14,1280,512]{2,1,0:T(8,128)(2,1)}, bf16[14,1280,512]{2,1,0:T(8,128)(2,1)}, bf16[14,1280,512]{2,...) custom-call(bf16[1024,5120]{1,0:T(8,128)(2,1)} %x.1, ...), custom_call_target="tpu_custom_call" | custom-call | flops 450971566080 | bytes 41943040 | tf_op jit(solution)/shard_map/pallas_call | solution.py:656
  1045.3 3.9 shard_map.47
